TPU v7x, 32 devices: a whole 2x2x4 slice. The times are simulated.
32 devices in a mesh: samp: 8 (over y, x, core), snp: 4 (over z).
Axes of the slice: x: 2, y: 2, z: 4, core: 2. Of those that a mesh axis runs over, the one named last changes fastest.
Arguments:
- genotypes: bfloat16 [8192, 16384], P('samp', 'snp'), may hold values from -6 to 6
- probes: bfloat16 [8, 8192], P(None, 'samp'), may hold values from -6 to 6
- env_label: int32 [8192], P('samp'), may hold values from 0 to 7
- variances: float32 [3], replicated, may hold values from 0.25 to 1
Outputs:
- first: float32 [8, 8192], P(None, 'samp')
- second: float32 [8, 8192], P(None, 'samp')
All inputs are finite; a program needn't handle non-finite values.
Results may differ from a plain program's by a relative error of at most 0.0018.
Values may be sent and summed in bfloat16 or wider, within the bound.
No kernel may reach another device: no remote copies, remote signals or barrier semaphores. Data moves between devices by JAX's collectives and lax.ppermute only.
A program may use at most 64 MiB of HBM per device.

v0:
```python
import jax
import jax.numpy as jnp
from jax import lax
from jax.sharding import PartitionSpec as P

SNPS = 16384
PROBES = 8
ENVS = 8


def local_image(snp_panel, genotypes):
    return lax.dot_general(
        snp_panel, genotypes, (((1,), (1,)), ((), ())), preferred_element_type=jnp.float32
    )


def apply_operator(current, genotypes, onehot, variances):
    rounded = current.astype(jnp.bfloat16)
    scaled = (onehot[:, None, :] * rounded[None, :, :]).reshape(ENVS * PROBES, -1)
    panel = jnp.concatenate([rounded, scaled], axis=0)
    partial_panel = jnp.dot(panel, genotypes, preferred_element_type=jnp.float32)
    snp_panel = lax.psum(partial_panel, "samp").astype(jnp.bfloat16)
    image = local_image(snp_panel, genotypes)
    additive = image[:PROBES]
    blocks = image[PROBES:].reshape(ENVS, PROBES, -1)
    interaction = jnp.sum(onehot.astype(jnp.float32)[:, None, :] * blocks, axis=0)
    weighted = variances[0] * additive / SNPS + variances[1] * interaction / SNPS
    totals = lax.psum(weighted, "snp")
    return totals + variances[2] * current


def per_device(genotypes, probes, env_label, variances):
    labels = jnp.arange(ENVS, dtype=jnp.int32)
    onehot = (env_label[None, :] == labels[:, None]).astype(jnp.bfloat16)
    first = apply_operator(probes.astype(jnp.float32), genotypes, onehot, variances)
    second = apply_operator(first, genotypes, onehot, variances)
    return (first, second)


def solution(mesh):
    return jax.shard_map(
        per_device,
        mesh=mesh,
        in_specs=(P("samp", "snp"), P(None, "samp"), P("samp"), P()),
        out_specs=(P(None, "samp"), P(None, "samp")),
        check_vma=False,
    )
```

profile of v0, /device:TPU:0, one launch (start us, length us, event | category | flops | bytes accessed | tf_op | source)
XLA Modules:
  0.0 167.7 jit_solution(6879203342592267592)
XLA Ops:
  0.6 1.4 fusion.25
  2.1 0.7 fusion.21
  2.8 0.7 multiply_bitcast_fusion.1
  3.5 5.0 %fusion.8 = f32[72,4096]{1,0:T(8,128)S(1)} fusion(bf16[1024,4096]{1,0:T(8,128)(2,1)} %param.4, bf16[64,1024]{1,0:T(8,128)(2,1)S(1)} %multiply_bitcast_fusion.1, bf16[8,1024]{1,0:T(8,128)(2,1)} %param.5), kind=kOutput, calls=%fused_computation.10 | convolution fusion | flops 604274688 | bytes 9715712 | tf_op jit(solution)/shard_map/dot_general | solution.py:21
  8.5 0.0 copy-start
  8.5 53.0 %all-reduce.2 = bf16[72,4096]{1,0:T(8,128)(2,1)S(1)} all-reduce(f32[72,4096]{1,0:T(8,128)S(1)} %fusion.8), channel_id=1, replica_groups=mesh['samp'=8,'snp'=4] {'samp'}, use_global_device_ids=true, to_apply=%region_0.0 | all-reduce | flops 294912 | bytes 1769472 | tf_op jit(solution)/shard_map/psum | solution.py:22
  61.5 6.0 %fusion.27 = f32[72,1024]{1,0:T(8,128)S(1)} fusion(bf16[72,4096]{1,0:T(8,128)(2,1)S(1)} %all-reduce.2, bf16[1024,4096]{1,0:T(8,128)(2,1)} %param.4), kind=kOutput, calls=%fused_computation.36 | convolution fusion | flops 603979776 | bytes 9273344 | tf_op jit(solution)/shard_map/dot_general | solution.py:12
  67.6 1.2 fusion.19
  68.8 19.5 %psum.29 = f32[8,1024]{1,0:T(8,128)S(1)} all-reduce(f32[8,1024]{1,0:T(8,128)S(1)} %fusion.19), channel_id=1, replica_groups=mesh['samp'=8,'snp'=4] {'snp'}, use_global_device_ids=true, to_apply=%region_2.0 | all-reduce | flops 8192 | bytes 65536 | tf_op jit(solution)/shard_map/psum | solution.py:28
  88.3 0.0 copy-done
  88.3 0.7 fusion.24
  89.0 0.0 copy-start.1
  89.1 5.0 %fusion.12 = f32[72,4096]{1,0:T(8,128)S(1)} fusion(bf16[1024,4096]{1,0:T(8,128)(2,1)} %param.4, bf16[64,1024]{1,0:T(8,128)(2,1)S(1)} %multiply_bitcast_fusion, bf16[8,1024]{1,0:T(8,128)(2,1)S(1)} %get-tuple-element.2), kind=kOutput, calls=%fused_computation.14 | convolution fusion | flops 604274688 | bytes 9715712 | tf_op jit(solution)/shard_map/dot_general | solution.py:21
  94.1 49.2 %all-reduce.3 = bf16[72,4096]{1,0:T(8,128)(2,1)S(1)} all-reduce(f32[72,4096]{1,0:T(8,128)S(1)} %fusion.12), channel_id=1, replica_groups=mesh['samp'=8,'snp'=4] {'samp'}, use_global_device_ids=true, to_apply=%region_3.0 | all-reduce | flops 294912 | bytes 1769472 | tf_op jit(solution)/shard_map/psum | solution.py:22
  143.3 6.0 %fusion.26 = f32[72,1024]{1,0:T(8,128)S(1)} fusion(bf16[72,4096]{1,0:T(8,128)(2,1)S(1)} %all-reduce.3, bf16[1024,4096]{1,0:T(8,128)(2,1)} %param.4), kind=kOutput, calls=%fused_computation.35 | convolution fusion | flops 603979776 | bytes 9273344 | tf_op jit(solution)/shard_map/dot_general | solution.py:12
  149.4 1.2 fusion.17
  150.6 15.8 %psum.31 = f32[8,1024]{1,0:T(8,128)S(1)} all-reduce(f32[8,1024]{1,0:T(8,128)S(1)} %fusion.17), channel_id=1, replica_groups=mesh['samp'=8,'snp'=4] {'snp'}, use_global_device_ids=true, to_apply=%region_5.0 | all-reduce | flops 8192 | bytes 65536 | tf_op jit(solution)/shard_map/psum | solution.py:28
  166.4 0.0 copy-done.1
  166.4 1.3 multiply_add_fusion
  (3 shorter events, 0.1 us)
Async XLA Ops:
  8.5 79.8 %copy-start = (bf16[8,1024]{1,0:T(8,128)(2,1)S(1)}, bf16[8,1024]{1,0:T(8,128)(2,1)}, u32[]{:S(2)}) copy-start(bf16[8,1024]{1,0:T(8,128)(2,1)} %param.5) | copy-start | bytes 49156
  89.0 77.4 %copy-start.1 = (f32[8,1024]{1,0:T(8,128)}, f32[8,1024]{1,0:T(8,128)S(1)}, u32[]{:S(2)}) copy-start(f32[8,1024]{1,0:T(8,128)S(1)} %get-tuple-element.3) | copy-start | bytes 98308
where the time goes:
time: 168 us
  blocking collectives  138 us (82%)
  matrix products  22.1 us (13%)
  other arithmetic  5.97 us (4%)
    psum x2, blocking collectives, apply_operator(): snp_panel = lax.psum(partial_panel, 'samp').astype(jnp.bfloat16)  102 us
    psum x2, blocking collectives, apply_operator(): totals = lax.psum(weighted, 'snp')  35.2 us
    dot_general x2, matrix products, local_image(): lax.dot_general(snp_panel, genotypes, (((1,), (1,)), ((), ())), preferred...  12.1 us
    dot_general x2, matrix products, apply_operator(): jnp.dot(panel, genotypes, preferred_element_type=jnp.float32)  9.96 us

commit v1 on v0

--- a/solution.py
+++ b/solution.py
@@ -25,7 +25,9 @@
     blocks = image[PROBES:].reshape(ENVS, PROBES, -1)
     interaction = jnp.sum(onehot.astype(jnp.float32)[:, None, :] * blocks, axis=0)
     weighted = variances[0] * additive / SNPS + variances[1] * interaction / SNPS
-    totals = lax.psum(weighted, "snp")
+    totals = weighted
+    for hop in (1, 2):
+        totals = totals + lax.ppermute(totals, "snp", [(dev, dev ^ hop) for dev in range(4)])
     return totals + variances[2] * current
 
 

time: 168 us -> 148 us (0.88)
  blocking collectives: 138 us -> 102 us
  waiting for transfers between devices: 0 us -> 9.13 us
  starting transfers between devices: 0 us -> 8.74 us
  matrix products: 22.1 us -> 18.9 us
    psum x2 -> x0, blocking collectives: 35.2 us -> none  [apply_operator(): totals = lax.psum(weighted, 'snp')]
    ppermute x0 -> x4, waiting for transfers between devices: none -> 9.13 us  [apply_operator(): lax.ppermute(totals, 'snp', [(dev, dev ^ hop) for dev in range(4)])]
    ppermute x0 -> x4, starting transfers between devices: none -> 8.74 us  [apply_operator(): lax.ppermute(totals, 'snp', [(dev, dev ^ hop) for dev in range(4)])]
    dot_general x2, matrix products: 9.96 us -> 6.62 us  [apply_operator(): jnp.dot(panel, genotypes, preferred_element_type=jnp.float32)]
  transfers between devices with their start and end apart: 0 -> 4, of which waited for: 0 -> 4; matrix products, arithmetic and copies ran while one was open for 0% -> 0% of each run, Pallas kernels for 0% -> 0%
where the time goes in v1:
time: 148 us; the launch traced here: 147 us
  blocking collectives  102 us (69%)
  matrix products  18.9 us (13%)
  waiting for transfers between devices  9.13 us (6%)
  starting transfers between devices  8.74 us (6%)
  other arithmetic  5.98 us (4%)
    psum x2, blocking collectives, apply_operator(): snp_panel = lax.psum(partial_panel, 'samp').astype(jnp.bfloat16)  102 us
    dot_general x2, matrix products, local_image(): lax.dot_general(snp_panel, genotypes, (((1,), (1,)), ((), ())), preferred...  12.2 us
    ppermute x4, waiting for transfers between devices, apply_operator(): lax.ppermute(totals, 'snp', [(dev, dev ^ hop) for dev in range(4)])  9.13 us
    ppermute x4, starting transfers between devices, apply_operator(): lax.ppermute(totals, 'snp', [(dev, dev ^ hop) for dev in range(4)])  8.74 us
    dot_general x2, matrix products, apply_operator(): jnp.dot(panel, genotypes, preferred_element_type=jnp.float32)  6.62 us
  transfers between devices with their start and end apart: 4, of which 4 were waited for; matrix products, arithmetic and copies ran while one was open for 0% of the time, Pallas kernels for 0%

profile of v1, /device:TPU:0, one launch (start us, length us, event | category | flops | bytes accessed | tf_op | source)
XLA Modules:
  0.0 147.3 jit_solution(5662917389011090696)
XLA Ops:
  0.6 1.4 fusion.25
  2.1 0.7 fusion.21
  2.8 0.7 multiply_bitcast_fusion.1
  3.5 5.0 %fusion.8 = f32[72,4096]{1,0:T(8,128)S(1)} fusion(bf16[1024,4096]{1,0:T(8,128)(2,1)} %param.4, bf16[64,1024]{1,0:T(8,128)(2,1)S(1)} %multiply_bitcast_fusion.1, bf16[8,1024]{1,0:T(8,128)(2,1)} %param.5), kind=kOutput, calls=%fused_computation.10 | convolution fusion | flops 604274688 | bytes 9715712 | tf_op jit(solution)/shard_map/dot_general | solution.py:21
  8.5 0.0 copy-start.1
  8.5 53.1 %all-reduce.2 = bf16[72,4096]{1,0:T(8,128)(2,1)S(1)} all-reduce(f32[72,4096]{1,0:T(8,128)S(1)} %fusion.8), channel_id=1, replica_groups=mesh['samp'=8,'snp'=4] {'samp'}, use_global_device_ids=true, to_apply=%region_0.0 | all-reduce | flops 294912 | bytes 1769472 | tf_op jit(solution)/shard_map/psum | solution.py:22
  61.6 0.0 copy-start
  61.6 6.2 %fusion.27 = f32[72,1024]{1,0:T(8,128)S(1)} fusion(bf16[72,4096]{1,0:T(8,128)(2,1)S(1)} %all-reduce.2, bf16[1024,4096]{1,0:T(8,128)(2,1)} %param.4), kind=kOutput, calls=%fused_computation.36 | convolution fusion | flops 603979776 | bytes 9273344 | tf_op jit(solution)/shard_map/dot_general | solution.py:12
  67.9 1.2 fusion.19
  69.1 1.7 %collective-permute-start = (f32[8,1024]{1,0:T(8,128)S(1)}, f32[8,1024]{1,0:T(8,128)S(1)}, u32[]{:S(2)}, u32[]{:S(2)}) collective-permute-start(f32[8,1024]{1,0:T(8,128)S(1)} %fusion.19), channel_id=1, source_target_pairs={{0,1},{1,0},{2,3},{3,2},{4,5},{5,4},{6,7},{7,6},{8,9},{9,8},{10,11... | collective-permute-start | bytes 98312 | tf_op jit(solution)/shard_map/ppermute | solution.py:30
  70.8 2.5 %collective-permute-done = f32[8,1024]{1,0:T(8,128)S(1)} collective-permute-done((f32[8,1024]{1,0:T(8,128)S(1)}, f32[8,1024]{1,0:T(8,128)S(1)}, u32[]{:S(2)}, u32[]{:S(2)}) %collective-permute-start) | collective-permute-done | bytes 32800 | tf_op jit(solution)/shard_map/ppermute | solution.py:30
  73.4 2.6 %collective-permute-start.1 = (f32[8,1024]{1,0:T(8,128)S(1)}, f32[8,1024]{1,0:T(8,128)S(1)}, u32[]{:S(2)}, u32[]{:S(2)}) collective-permute-start(f32[8,1024]{1,0:T(8,128)S(1)} %add.31), channel_id=1, source_target_pairs={{0,2},{1,3},{2,0},{3,1},{4,6},{5,7},{6,4},{7,5},{8,10},{9,11},{10,... | collective-permute-start | bytes 98312 | tf_op jit(solution)/shard_map/ppermute | solution.py:30
  75.9 2.2 %collective-permute-done.1 = f32[8,1024]{1,0:T(8,128)S(1)} collective-permute-done((f32[8,1024]{1,0:T(8,128)S(1)}, f32[8,1024]{1,0:T(8,128)S(1)}, u32[]{:S(2)}, u32[]{:S(2)}) %collective-permute-start.1) | collective-permute-done | bytes 32800 | tf_op jit(solution)/shard_map/ppermute | solution.py:30
  78.2 0.7 fusion.24
  78.9 0.0 copy-start.2
  78.9 1.6 %fusion.12 = f32[72,4096]{1,0:T(8,128)S(1)} fusion(bf16[1024,4096]{1,0:T(8,128)(2,1)S(1)} %copy-done, bf16[64,1024]{1,0:T(8,128)(2,1)S(1)} %multiply_bitcast_fusion, bf16[8,1024]{1,0:T(8,128)(2,1)S(1)} %get-tuple-element.2), kind=kOutput, calls=%fused_computation.14 | convolution fusion | flops 604274688 | bytes 9715712 | tf_op jit(solution)/shard_map/dot_general | solution.py:21
  80.6 49.2 %all-reduce.3 = bf16[72,4096]{1,0:T(8,128)(2,1)S(1)} all-reduce(f32[72,4096]{1,0:T(8,128)S(1)} %fusion.12), channel_id=1, replica_groups=mesh['samp'=8,'snp'=4] {'samp'}, use_global_device_ids=true, to_apply=%region_2.0 | all-reduce | flops 294912 | bytes 1769472 | tf_op jit(solution)/shard_map/psum | solution.py:22
  129.8 6.0 %fusion.26 = f32[72,1024]{1,0:T(8,128)S(1)} fusion(bf16[72,4096]{1,0:T(8,128)(2,1)S(1)} %all-reduce.3, bf16[1024,4096]{1,0:T(8,128)(2,1)} %param.4), kind=kOutput, calls=%fused_computation.35 | convolution fusion | flops 603979776 | bytes 9273344 | tf_op jit(solution)/shard_map/dot_general | solution.py:12
  135.9 1.2 fusion.17
  137.1 1.8 %collective-permute-start.2 = (f32[8,1024]{1,0:T(8,128)S(1)}, f32[8,1024]{1,0:T(8,128)S(1)}, u32[]{:S(2)}, u32[]{:S(2)}) collective-permute-start(f32[8,1024]{1,0:T(8,128)S(1)} %fusion.17), channel_id=1, source_target_pairs={{0,1},{1,0},{2,3},{3,2},{4,5},{5,4},{6,7},{7,6},{8,9},{9,8},{10,11... | collective-permute-start | bytes 98312 | tf_op jit(solution)/shard_map/ppermute | solution.py:30
  138.9 2.2 %collective-permute-done.2 = f32[8,1024]{1,0:T(8,128)S(1)} collective-permute-done((f32[8,1024]{1,0:T(8,128)S(1)}, f32[8,1024]{1,0:T(8,128)S(1)}, u32[]{:S(2)}, u32[]{:S(2)}) %collective-permute-start.2) | collective-permute-done | bytes 32800 | tf_op jit(solution)/shard_map/ppermute | solution.py:30
  141.1 2.6 %collective-permute-start.3 = (f32[8,1024]{1,0:T(8,128)S(1)}, f32[8,1024]{1,0:T(8,128)S(1)}, u32[]{:S(2)}, u32[]{:S(2)}) collective-permute-start(f32[8,1024]{1,0:T(8,128)S(1)} %add.35), channel_id=1, source_target_pairs={{0,2},{1,3},{2,0},{3,1},{4,6},{5,7},{6,4},{7,5},{8,10},{9,11},{10,... | collective-permute-start | bytes 98312 | tf_op jit(solution)/shard_map/ppermute | solution.py:30
  143.8 2.2 %collective-permute-done.3 = f32[8,1024]{1,0:T(8,128)S(1)} collective-permute-done((f32[8,1024]{1,0:T(8,128)S(1)}, f32[8,1024]{1,0:T(8,128)S(1)}, u32[]{:S(2)}, u32[]{:S(2)}) %collective-permute-start.3) | collective-permute-done | bytes 32800 | tf_op jit(solution)/shard_map/ppermute | solution.py:30
  145.9 1.3 multiply_add_fusion
  (8 shorter events, 0.1 us)
Async XLA Ops:
  8.5 69.7 %copy-start.1 = (bf16[8,1024]{1,0:T(8,128)(2,1)S(1)}, bf16[8,1024]{1,0:T(8,128)(2,1)}, u32[]{:S(2)}) copy-start(bf16[8,1024]{1,0:T(8,128)(2,1)} %param.5) | copy-start | bytes 49156
  61.6 17.3 %copy-start = (bf16[1024,4096]{1,0:T(8,128)(2,1)S(1)}, bf16[1024,4096]{1,0:T(8,128)(2,1)}, u32[]{:S(2)}) copy-start(bf16[1024,4096]{1,0:T(8,128)(2,1)} %param.4) | copy-start | bytes 25165828
  69.1 4.3 %collective-permute-start = (f32[8,1024]{1,0:T(8,128)S(1)}, f32[8,1024]{1,0:T(8,128)S(1)}, u32[]{:S(2)}, u32[]{:S(2)}) collective-permute-start(f32[8,1024]{1,0:T(8,128)S(1)} %fusion.19), channel_id=1, source_target_pairs={{0,1},{1,0},{2,3},{3,2},{4,5},{5,4},{6,7},{7,6},{8,9},{9,8},{10,11... | collective-permute-start | bytes 98312 | tf_op jit(solution)/shard_map/ppermute | solution.py:30
  73.4 4.8 %collective-permute-start.1 = (f32[8,1024]{1,0:T(8,128)S(1)}, f32[8,1024]{1,0:T(8,128)S(1)}, u32[]{:S(2)}, u32[]{:S(2)}) collective-permute-start(f32[8,1024]{1,0:T(8,128)S(1)} %add.31), channel_id=1, source_target_pairs={{0,2},{1,3},{2,0},{3,1},{4,6},{5,7},{6,4},{7,5},{8,10},{9,11},{10,... | collective-permute-start | bytes 98312 | tf_op jit(solution)/shard_map/ppermute | solution.py:30
  78.9 67.1 %copy-start.2 = (f32[8,1024]{1,0:T(8,128)}, f32[8,1024]{1,0:T(8,128)S(1)}, u32[]{:S(2)}) copy-start(f32[8,1024]{1,0:T(8,128)S(1)} %get-tuple-element.3) | copy-start | bytes 98308
  137.1 4.0 %collective-permute-start.2 = (f32[8,1024]{1,0:T(8,128)S(1)}, f32[8,1024]{1,0:T(8,128)S(1)}, u32[]{:S(2)}, u32[]{:S(2)}) collective-permute-start(f32[8,1024]{1,0:T(8,128)S(1)} %fusion.17), channel_id=1, source_target_pairs={{0,1},{1,0},{2,3},{3,2},{4,5},{5,4},{6,7},{7,6},{8,9},{9,8},{10,11... | collective-permute-start | bytes 98312 | tf_op jit(solution)/shard_map/ppermute | solution.py:30
  141.1 4.8 %collective-permute-start.3 = (f32[8,1024]{1,0:T(8,128)S(1)}, f32[8,1024]{1,0:T(8,128)S(1)}, u32[]{:S(2)}, u32[]{:S(2)}) collective-permute-start(f32[8,1024]{1,0:T(8,128)S(1)} %add.35), channel_id=1, source_target_pairs={{0,2},{1,3},{2,0},{3,1},{4,6},{5,7},{6,4},{7,5},{8,10},{9,11},{10,... | collective-permute-start | bytes 98312 | tf_op jit(solution)/shard_map/ppermute | solution.py:30
